TPU v7x, 32 devices: a whole 2x2x4 slice. The times are simulated.
32 devices in a mesh: seq: 8 (over z, x), head: 4 (over y, core).
Axes of the slice: x: 2, y: 2, z: 4, core: 2. Of those that a mesh axis runs over, the one named last changes fastest.
Arguments:
- queries: bfloat16 [8, 64, 128], P('seq', 'head'), may hold values from -90 to 90
- keys: bfloat16 [8, 8, 4096, 128], P(None, 'head', 'seq'), may hold values from -4 to 4
- values: bfloat16 [8, 8, 4096, 128], P(None, 'head', 'seq'), may hold values from -6 to 6
- old_scores: float32 [8, 8, 4096], P(None, 'head', 'seq'), may hold values from 0 to 4
- lengths: int32 [8], replicated, may hold values from 1024 to 4096
- valid_counts: int32 [8, 32], P(None, 'seq'), may hold values from 1 to 128
Outputs:
- attended: bfloat16 [8, 64, 128], P('seq', 'head')
- heavy_scores: float32 [8, 8, 4096], P(None, 'head', 'seq')
Inputs may be any that keep to these rules, and one draw needn't show every extreme that they name: `lengths`: slot c of a sequence is cached when c is below its length. `valid_counts`: in block k of a sequence, the slots k * 128 + j with j below the count are live and the others are evicted.
All inputs are finite; a program needn't handle non-finite values.
Results may differ from a plain program's by a relative error of at most 0.0075.
Values may be sent and summed in bfloat16 or wider, within the bound.
A program may use at most 64 MiB of HBM per device.

v0:
```python
import jax
import jax.numpy as jnp
from jax import lax
from jax.sharding import PartitionSpec as P

HD = 128
BLK = 128


def on_device(queries, keys, values, old_scores, lengths, valid_counts):
    seq_dev = queries.shape[0]
    kv_local = keys.shape[1]
    ctx_dev = keys.shape[2]
    gathered = lax.all_gather(queries, "seq", axis=0, tiled=True)
    seq_count = gathered.shape[0]
    group_size = gathered.shape[1] // kv_local
    grouped = gathered.reshape(seq_count, kv_local, group_size, HD)
    scores = jnp.einsum(
        "bhgd,bhcd->bhgc", grouped, keys, preferred_element_type=jnp.float32
    ) * HD ** (-0.5)
    offset = lax.axis_index("seq") * ctx_dev
    position = offset + jnp.arange(ctx_dev, dtype=jnp.int32)
    block_slot = jnp.arange(BLK, dtype=jnp.int32)
    in_block = (valid_counts[:, :, None] > block_slot[None, None, :]).reshape(seq_count, ctx_dev)
    live_mask = (position[None, :] < lengths[:, None]) & in_block
    masked = jnp.where(live_mask[:, None, None, :], scores, -jnp.inf)
    local_top = jnp.max(masked, axis=3)
    has_live = local_top > -jnp.inf
    local_safe = jnp.where(has_live, local_top, 0.0)
    exponent = jnp.exp(masked - local_safe[:, :, :, None])
    weights = exponent.astype(jnp.bfloat16)
    partial_mixed = jnp.einsum(
        "bhgc,bhcd->bhgd", weights, values, preferred_element_type=jnp.float32
    )
    partial_total = jnp.sum(exponent, axis=3)
    recv_mixed, recv_total, recv_top = (
        lax.all_to_all(partial_mixed, "seq", split_axis=0, concat_axis=0, tiled=True),
        lax.all_to_all(partial_total, "seq", split_axis=0, concat_axis=0, tiled=True),
        lax.all_to_all(local_top, "seq", split_axis=0, concat_axis=0, tiled=True),
    )
    sources = recv_top.shape[0] // seq_dev
    recv_mixed = recv_mixed.reshape(sources, seq_dev, kv_local, group_size, HD)
    recv_total = recv_total.reshape(sources, seq_dev, kv_local, group_size)
    recv_top = recv_top.reshape(sources, seq_dev, kv_local, group_size)
    own_top = jnp.max(recv_top, axis=0)
    factor = jnp.exp(recv_top - own_top[None])
    own_mixed = jnp.sum(factor[:, :, :, :, None] * recv_mixed, axis=0)
    own_total = jnp.sum(factor * recv_total, axis=0)
    row_top, row_total = (
        lax.all_gather(own_top, "seq", axis=0, tiled=True),
        lax.all_gather(own_total, "seq", axis=0, tiled=True),
    )
    rescale = jnp.where(has_live, jnp.exp(local_safe - row_top), 0.0) / row_total
    heavy_scores = old_scores + jnp.sum(exponent * rescale[:, :, :, None], axis=2)
    attended = (own_mixed / own_total[:, :, :, None]).astype(jnp.bfloat16)
    attended = attended.reshape(seq_dev, kv_local * group_size, HD)
    return (attended, heavy_scores)


def solution(mesh):
    return jax.shard_map(
        on_device,
        mesh=mesh,
        in_specs=(
            P("seq", "head", None),
            P(None, "head", "seq", None),
            P(None, "head", "seq", None),
            P(None, "head", "seq"),
            P(),
            P(None, "seq"),
        ),
        out_specs=(P("seq", "head", None), P(None, "head", "seq")),
        check_vma=False,
    )
```

profile of v0, /device:TPU:0, one launch (start us, length us, event | category | flops | bytes accessed | tf_op | source)
XLA Modules:
  0.0 100.4 jit_solution(8737390993984472409)
XLA Ops:
  0.6 0.0 copy-start
  0.7 32.7 %all_gather.9 = bf16[8,16,128]{2,1,0:T(8,128)(2,1)S(1)} all-gather(bf16[1,16,128]{2,1,0:T(8,128)(2,1)} %param.6), channel_id=1, replica_groups=mesh['seq'=8,'head'=4] {'seq'}, dimensions={0}, use_global_device_ids=true | all-gather | bytes 36864 | tf_op jit(solution)/shard_map/all_gather | solution.py:14
  33.4 0.8 fusion.7
  34.1 0.0 copy-done
  34.1 1.3 %fusion.10 = (f32[8,2,8]{2,1,0:T(2,128)}, f32[8,2,8,512]{3,2,1,0:T(8,128)S(1)}) fusion(bf16[8,2,512,128]{3,2,1,0:T(8,128)(2,1)S(1)} %copy-done, bf16[8,16,128]{2,1,0:T(8,128)(2,1)S(1)} %all_gather.9, pred[8,512]{1,0:T(8,128)(4,1)S(1)} %fusion.7), kind=kOutput, calls=%fused_computation.21 | convolution fusion | flops 16973696 | bytes 2396672 | tf_op jit(solution)/shard_map/bhgd,bhcd->bhgc/dot_general | solution.py:18
  35.5 0.0 copy-start.1
  35.5 5.6 %all-to-all-start = ((f32[8,2,8]{2,1,0:T(2,128)}), f32[8,2,8]{2,1,0:T(2,128)S(1)}, u32[]{:S(2)}, u32[]{:S(2)}) async-start(f32[8,2,8]{2,1,0:T(2,128)} %get-tuple-element.4), calls=%async_computation | async-start | bytes 16384 | tf_op jit(solution)/shard_map/all_to_all | solution.py:39
  41.1 0.7 compare_select_fusion.1
  41.8 0.8 fusion.1
  42.6 5.0 %all-to-all-done = f32[8,2,8]{2,1,0:T(2,128)S(1)} async-done(((f32[8,2,8]{2,1,0:T(2,128)}), f32[8,2,8]{2,1,0:T(2,128)S(1)}, u32[]{:S(2)}, u32[]{:S(2)}) %all-to-all-start) | async-done | bytes 544 | tf_op jit(solution)/shard_map/all_to_all | solution.py:39
  47.6 3.3 %all-to-all-start.2 = ((f32[8,2,8]{2,1,0:T(2,128)}), f32[8,2,8]{2,1,0:T(2,128)S(1)}, u32[]{:S(2)}, u32[]{:S(2)}) async-start(f32[8,2,8]{2,1,0:T(2,128)} %fusion.1), calls=%async_computation.2 | async-start | bytes 16384 | tf_op jit(solution)/shard_map/all_to_all | solution.py:38
  50.9 2.7 %fusion.3 = f32[8,2,8,128]{3,2,1,0:T(8,128)} fusion(bf16[8,2,512,128]{3,2,1,0:T(8,128)(2,1)} %param.8, f32[8,2,8,512]{3,2,1,0:T(8,128)S(1)} %get-tuple-element.5, f32[8,2,8]{2,1,0:T(2,128)S(1)} %compare_select_fusion.1), kind=kOutput, calls=%fused_computation.6 | convolution fusion | flops 16908288 | bytes 2425344 | tf_op jit(solution)/shard_map/bhgc,bhcd->bhgd/dot_general | solution.py:32
  53.6 3.8 %all-to-all-done.2 = f32[8,2,8]{2,1,0:T(2,128)S(1)} async-done(((f32[8,2,8]{2,1,0:T(2,128)}), f32[8,2,8]{2,1,0:T(2,128)S(1)}, u32[]{:S(2)}, u32[]{:S(2)}) %all-to-all-start.2) | async-done | bytes 544 | tf_op jit(solution)/shard_map/all_to_all | solution.py:38
  57.4 3.3 %all-to-all-start.1 = ((f32[8,2,8,128]{3,2,1,0:T(8,128)}), f32[8,2,8,128]{3,2,1,0:T(8,128)S(1)}, u32[]{:S(2)}, u32[]{:S(2)}) async-start(f32[8,2,8,128]{3,2,1,0:T(8,128)} %fusion.3), calls=%async_computation.1 | async-start | bytes 131072 | tf_op jit(solution)/shard_map/all_to_all | solution.py:37
  60.8 0.1 div.22
  60.9 20.9 %all-gather.2 = f32[8,2,8]{2,1,0:T(2,128)S(1)} all-gather(f32[1,2,8]{2,1,0:T(2,128)S(1)} %bitcast.19), channel_id=2, replica_groups=mesh['seq'=8,'head'=4] {'seq'}, dimensions={0}, use_global_device_ids=true | all-gather | bytes 576 | tf_op jit(solution)/shard_map/all_gather | solution.py:50
  81.8 16.3 %all-gather.3 = f32[8,2,8]{2,1,0:T(2,128)S(1)} all-gather(f32[1,2,8]{2,1,0:T(2,128)S(1)} %bitcast.20), channel_id=3, replica_groups=mesh['seq'=8,'head'=4] {'seq'}, dimensions={0}, use_global_device_ids=true | all-gather | bytes 576 | tf_op jit(solution)/shard_map/all_gather | solution.py:51
  98.1 0.7 fusion.8
  98.8 0.2 multiply_reduce_fusion
  99.0 0.0 copy-done.1
  99.0 0.6 add.15
  99.6 0.0 all-to-all-done.1
  99.6 0.1 multiply_reduce_fusion.1
  99.7 0.7 fusion.9
  (4 shorter events, 0.1 us)
Async XLA Ops:
  0.6 33.5 %copy-start = (bf16[8,2,512,128]{3,2,1,0:T(8,128)(2,1)S(1)}, bf16[8,2,512,128]{3,2,1,0:T(8,128)(2,1)}, u32[]{:S(2)}) copy-start(bf16[8,2,512,128]{3,2,1,0:T(8,128)(2,1)} %param.7) | copy-start | bytes 6291460
  35.5 63.5 %copy-start.1 = (f32[8,2,512]{2,1,0:T(2,128)S(1)}, f32[8,2,512]{2,1,0:T(2,128)}, u32[]{:S(2)}) copy-start(f32[8,2,512]{2,1,0:T(2,128)} %param.9) | copy-start | bytes 98308
  35.5 12.1 %all-to-all-start = ((f32[8,2,8]{2,1,0:T(2,128)}), f32[8,2,8]{2,1,0:T(2,128)S(1)}, u32[]{:S(2)}, u32[]{:S(2)}) async-start(f32[8,2,8]{2,1,0:T(2,128)} %get-tuple-element.4), calls=%async_computation | async-start | bytes 16384 | tf_op jit(solution)/shard_map/all_to_all | solution.py:39
  47.6 9.8 %all-to-all-start.2 = ((f32[8,2,8]{2,1,0:T(2,128)}), f32[8,2,8]{2,1,0:T(2,128)S(1)}, u32[]{:S(2)}, u32[]{:S(2)}) async-start(f32[8,2,8]{2,1,0:T(2,128)} %fusion.1), calls=%async_computation.2 | async-start | bytes 16384 | tf_op jit(solution)/shard_map/all_to_all | solution.py:38
  57.4 42.2 %all-to-all-start.1 = ((f32[8,2,8,128]{3,2,1,0:T(8,128)}), f32[8,2,8,128]{3,2,1,0:T(8,128)S(1)}, u32[]{:S(2)}, u32[]{:S(2)}) async-start(f32[8,2,8,128]{3,2,1,0:T(8,128)} %fusion.3), calls=%async_computation.1 | async-start | bytes 131072 | tf_op jit(solution)/shard_map/all_to_all | solution.py:37
where the time goes:
time: 101 us; the launch traced here: 100 us
  blocking collectives  69.9 us (69%)
  starting transfers between devices  12.2 us (12%)
  waiting for transfers between devices  8.82 us (9%)
  other arithmetic  4.62 us (5%)
  matrix products  4 us (4%)
    all_gather x1, blocking collectives, on_device(): gathered = lax.all_gather(queries, 'seq', axis=0, tiled=True)  32.7 us
    all_gather x1, blocking collectives, on_device(): lax.all_gather(own_top, 'seq', axis=0, tiled=True)  20.9 us
    all_gather x1, blocking collectives, on_device(): lax.all_gather(own_total, 'seq', axis=0, tiled=True)  16.3 us
    all_to_all x1, starting transfers between devices, on_device(): lax.all_to_all(local_top, 'seq', split_axis=0, concat_axis=0, tiled=True)  5.59 us
    all_to_all x1, waiting for transfers between devices, on_device(): lax.all_to_all(local_top, 'seq', split_axis=0, concat_axis=0, tiled=True)  4.99 us
    all_to_all x1, waiting for transfers between devices, on_device(): lax.all_to_all(partial_total, 'seq', split_axis=0, concat_axis=0, tiled=T...  3.83 us
    all_to_all x1, starting transfers between devices, on_device(): lax.all_to_all(partial_mixed, 'seq', split_axis=0, concat_axis=0, tiled=T...  3.35 us
    all_to_all x1, starting transfers between devices, on_device(): lax.all_to_all(partial_total, 'seq', split_axis=0, concat_axis=0, tiled=T...  3.29 us
  transfers between devices with their start and end apart: 3, of which 2 were waited for; matrix products, arithmetic and copies ran while one was open for 6% of the time, Pallas kernels for 0%

commit v1 on v0

v1 whole, which is shorter than its diff:
```python
import functools

import jax
import jax.numpy as jnp
from jax import lax
from jax.experimental import pallas as pl
from jax.experimental.pallas import tpu as pltpu
from jax.sharding import PartitionSpec as P

BLK = 128
LANES = 128
NEG = -1e30
MESH = pl.DeviceIdType.MESH


def flipped(me, code):
    out = me
    bit = 1
    while bit <= code:
        if code & bit:
            out = out + bit * (1 - 2 * ((me // bit) % 2))
        bit *= 2
    return out


def kernel(n, kv, group, ctx, q_hbm, k_hbm, v_hbm, old_hbm, len_hbm, cnt_hbm,
           att_ref, heavy_ref,
           q_all, k_all, v_all, old_all, len_s, cnt_s, prob, part_out, part_in, stat,
           q_dma, k_dma, v_dma, misc_dma, q_send, q_recv, p_send, p_recv, s_send, s_recv):
    me = lax.axis_index("seq")
    rows = kv * group
    blocks = ctx // BLK
    stat_rows = (n * rows) // LANES
    hd = q_all.shape[-1]
    scale = hd ** -0.5
    seqs = [flipped(me, c) for c in range(n)]

    barrier = pltpu.get_barrier_semaphore()
    for c in range(1, n):
        pl.semaphore_signal(barrier, inc=1, device_id={"seq": seqs[c]}, device_id_type=MESH)

    q_copy = pltpu.make_async_copy(q_hbm.at[0], q_all.at[0], q_dma)
    q_copy.start()
    len_copy = pltpu.make_async_copy(len_hbm, len_s, misc_dma.at[0])
    len_copy.start()
    cnt_copy = pltpu.make_async_copy(cnt_hbm, cnt_s, misc_dma.at[1])
    cnt_copy.start()
    k_copies = [pltpu.make_async_copy(k_hbm.at[seqs[c]], k_all.at[c], k_dma.at[c]) for c in range(n)]
    v_copies = [pltpu.make_async_copy(v_hbm.at[seqs[c]], v_all.at[c], v_dma.at[c]) for c in range(n)]
    for c in range(n):
        k_copies[c].start()
        v_copies[c].start()
    old_copy = pltpu.make_async_copy(old_hbm, old_all, misc_dma.at[2])
    old_copy.start()

    q_copy.wait()
    pl.semaphore_wait(barrier, n - 1)

    def to_peer(src, dst, send_sem, recv_sem, c):
        return pltpu.make_async_remote_copy(
            src_ref=src, dst_ref=dst, send_sem=send_sem, recv_sem=recv_sem,
            device_id={"seq": seqs[c]}, device_id_type=MESH)

    q_sends = [to_peer(q_all.at[0], q_all.at[c], q_send.at[c], q_recv.at[c], c) for c in range(1, n)]
    for copy in reversed(q_sends):
        copy.start()

    lane = lax.broadcasted_iota(jnp.int32, (group, LANES), 1)
    sub = lax.broadcasted_iota(jnp.int32, (group, LANES), 0)
    lane_pair = lane // group
    per_row = LANES // group
    tops = [jnp.zeros((group, LANES), jnp.float32) for _ in range(stat_rows)]
    totals = [jnp.zeros((group, LANES), jnp.float32) for _ in range(stat_rows)]

    len_copy.wait()
    cnt_copy.wait()
    p_sends = []
    half = max(n // 2, 1)
    steps = [list(range(0, 1)), list(range(1, half)), list(range(half, n))]
    for codes in steps:
        for c in codes:
            if c:
                q_sends[c - 1].wait_recv()
            k_copies[c].wait()
            v_copies[c].wait()
        raw = {}
        for c in codes:
            for g in range(kv):
                full = lax.dot_general(q_all[c], k_all[c, g], (((1,), (1,)), ((), ())),
                                       preferred_element_type=jnp.float32)
                raw[c, g] = full[g * group:(g + 1) * group] * scale
        tight = {}
        for c in codes:
            b = seqs[c]
            seen = len_s[b] - me * ctx
            limits = [jnp.minimum(cnt_s[k, b], seen - k * BLK) for k in range(blocks)]
            for g in range(kv):
                masked = jnp.concatenate(
                    [jnp.where(lane < limits[k], raw[c, g][:, k * BLK:(k + 1) * BLK], NEG)
                     for k in range(blocks)], axis=1)
                top = jnp.max(masked, axis=1, keepdims=True)
                p = jnp.exp(masked - top)
                prob[c, g] = p
                total = jnp.sum(p, axis=1, keepdims=True)
                tight[c, g] = p
                pair = b * kv + g
                for r in range(stat_rows):
                    here = lane_pair == pair - r * per_row
                    tops[r] = jnp.where(here, top, tops[r])
                    totals[r] = jnp.where(here, total, totals[r])
        for c in codes:
            wide = jnp.concatenate([tight[c, g] for g in range(kv)], axis=0).astype(jnp.bfloat16)
            mixed = jnp.concatenate(
                [jnp.dot(wide, v_all[c, g], preferred_element_type=jnp.float32)[g * group:(g + 1) * group]
                 for g in range(kv)], axis=0)
            if c:
                part_out[c] = mixed
            else:
                part_in[0] = mixed
        if codes is steps[-1]:
            diag = (lane % group) == sub
            for r in range(stat_rows):
                stat[0, r:r + 1, :] = jnp.sum(jnp.where(diag, tops[r], 0.0), axis=0, keepdims=True)
                stat[0, stat_rows + r:stat_rows + r + 1, :] = jnp.sum(
                    jnp.where(diag, totals[r], 0.0), axis=0, keepdims=True)
        for c in codes:
            if c:
                copy = to_peer(part_out.at[c], part_in.at[c], p_send.at[c], p_recv.at[c], c)
                copy.start()
                p_sends.append(copy)

    s_sends = [to_peer(stat.at[0], stat.at[c], s_send.at[c], s_recv.at[c], c) for c in range(1, n)]
    for copy in reversed(s_sends):
        copy.start()
    old_copy.wait()
    for copy in s_sends:
        copy.wait_recv()

    fac = [[None] * stat_rows for _ in range(n)]
    for r in range(stat_rows):
        top_rows = [jnp.broadcast_to(stat[c, r:r + 1, :], (group, LANES)) for c in range(n)]
        tot_rows = [jnp.broadcast_to(stat[c, stat_rows + r:stat_rows + r + 1, :], (group, LANES)) for c in range(n)]
        best = functools.reduce(jnp.maximum, top_rows)
        scaled = [jnp.exp(t - best) for t in top_rows]
        whole = functools.reduce(jnp.add, [f * t for f, t in zip(scaled, tot_rows)])
        for c in range(n):
            fac[c][r] = scaled[c] / whole

    def column(row_list, pair):
        kept = [jnp.where(lane == pair * group - r * LANES + sub, row_list[r], 0.0)
                for r in range(stat_rows)]
        return jnp.sum(functools.reduce(jnp.add, kept), axis=1, keepdims=True)

    for c in range(n):
        b = seqs[c]
        for g in range(kv):
            share = column(fac[0], b * kv + g)
            add = jnp.sum(prob[c, g] * share, axis=0, keepdims=True)
            heavy_ref[b, g:g + 1, :] = old_all[b, g:g + 1, :] + add

    shares = [jnp.concatenate([column(fac[c], me * kv + g) for g in range(kv)], axis=0) for c in range(n)]
    for copy in p_sends:
        copy.wait_recv()
    att_ref[0] = functools.reduce(
        jnp.add, [shares[c] * part_in[c] for c in range(n)]).astype(jnp.bfloat16)
    for copy in q_sends + p_sends + s_sends:
        copy.wait_send()


def on_device(n, queries, keys, values, old_scores, lengths, valid_counts):
    own, rows, hd = queries.shape
    _, kv, ctx, _ = keys.shape
    group = rows // kv
    assert own == 1 and n & (n - 1) == 0 and (n * rows) % LANES == 0
    counts = valid_counts.T
    stat_rows = (n * rows) // LANES
    anywhere = pl.BlockSpec(memory_space=pl.ANY)
    vmem = pl.BlockSpec(memory_space=pltpu.VMEM)
    dma = pltpu.SemaphoreType.DMA
    return pl.pallas_call(
        functools.partial(kernel, n, kv, group, ctx),
        out_shape=(jax.ShapeDtypeStruct((own, rows, hd), jnp.bfloat16),
                   jax.ShapeDtypeStruct(old_scores.shape, jnp.float32)),
        in_specs=[anywhere] * 6,
        out_specs=(vmem, vmem),
        scratch_shapes=[
            pltpu.VMEM((n, rows, hd), jnp.bfloat16),
            pltpu.VMEM((n, kv, ctx, hd), jnp.bfloat16),
            pltpu.VMEM((n, kv, ctx, hd), jnp.bfloat16),
            pltpu.VMEM(old_scores.shape, jnp.float32),
            pltpu.SMEM(lengths.shape, jnp.int32),
            pltpu.SMEM(counts.shape, jnp.int32),
            pltpu.VMEM((n, kv, group, ctx), jnp.float32),
            pltpu.VMEM((n, rows, hd), jnp.float32),
            pltpu.VMEM((n, rows, hd), jnp.float32),
            pltpu.VMEM((n, 2 * stat_rows, LANES), jnp.float32),
            dma, dma((n,)), dma((n,)), dma((3,)),
            dma((n,)), dma((n,)), dma((n,)), dma((n,)), dma((n,)), dma((n,)),
        ],
        compiler_params=pltpu.CompilerParams(collective_id=0, has_side_effects=True),
    )(queries, keys, values, old_scores, lengths, counts)


def solution(mesh):
    return jax.shard_map(
        functools.partial(on_device, mesh.shape["seq"]),
        mesh=mesh,
        in_specs=(
            P("seq", "head", None),
            P(None, "head", "seq", None),
            P(None, "head", "seq", None),
            P(None, "head", "seq"),
            P(),
            P(None, "seq"),
        ),
        out_specs=(P("seq", "head", None), P(None, "head", "seq")),
        check_vma=False,
    )
```

time: 101 us -> 20 us (0.20)
  blocking collectives: 69.9 us -> 0 us
  Pallas kernels: 0 us -> 16.5 us
  starting transfers between devices: 12.2 us -> 0 us
  waiting for transfers between devices: 8.82 us -> 0 us
  other arithmetic: 4.62 us -> 0 us
  matrix products: 4 us -> 0 us
  local copies, waits for them, and re-layouts: 0.1 us -> 2.65 us
    all_gather x3 -> x0, blocking collectives: 69.9 us -> none  [the longest x1 32.7 us: on_device(): gathered = lax.all_gather(queries, 'seq', axis=0, tiled=True)]
    pallas_call x0 -> x1, Pallas kernels: none -> 16.5 us  [on_device(): pl.pallas_call(functools.partial(kernel, n, kv, group, ctx), out_shape=(j...]
    all_to_all x3 -> x0, starting transfers between devices: 12.2 us -> none  [the longest x1 5.59 us: on_device(): lax.all_to_all(local_top, 'seq', split_axis=0, concat_axis=0, tiled=True)]
    all_to_all x3 -> x0, waiting for transfers between devices: 8.82 us -> none  [the longest x1 4.99 us: on_device(): lax.all_to_all(local_top, 'seq', split_axis=0, concat_axis=0, tiled=True)]
    dot_general x2 -> x0, matrix products: 4 us -> none  [the longest x1 2.66 us: on_device(): jnp.einsum('bhgc,bhcd->bhgd', weights, values, preferred_element_type=jnp...]
    unnamed x4 -> x2, local copies, waits for them, and re-layouts: 0.01 us -> 2.65 us
    reduce_sum x4 -> x0, other arithmetic: 1.08 us -> none  [the longest x1 0.79 us: on_device(): partial_total = jnp.sum(exponent, axis=3)]
  transfers between devices with their start and end apart: 3 -> 0, of which waited for: 2 -> 0; matrix products, arithmetic and copies ran while one was open for 6% -> 0% of each run, Pallas kernels for 0% -> 0%
where the time goes in v1:
time: 20 us; the launch traced here: 19.8 us
  Pallas kernels  16.5 us (82%)
  local copies, waits for them, and re-layouts  2.65 us (13%)
  between operations  0.64 us (3%)
    pallas_call x1, Pallas kernels, on_device(): pl.pallas_call(functools.partial(kernel, n, kv, group, ctx), out_shape=(j...  16.5 us
    unnamed x2, local copies, waits for them, and re-layouts  2.65 us

profile of v1, /device:TPU:0, one launch (start us, length us, event | category | flops | bytes accessed | tf_op | source)
XLA Modules:
  0.0 19.8 jit_solution(14160695842098474311)
XLA Ops:
  0.6 16.5 %shard_map.77 = (bf16[1,16,128]{2,1,0:T(8,128)(2,1)}, f32[8,2,512]{2,1,0:T(2,128)}) custom-call(bf16[1,16,128]{2,1,0:T(8,128)(2,1)} %q_hbm.1, bf16[8,2,512,128]{3,2,1,0:T(8,128)(2,1)} %k_hbm.1, bf16[8,2,512,128]{3,2,1,0:T(8,128)(2,1)} %v_hbm.1, f32[8,2,512]{2,1,0:T(2,128)} %old_hbm.1, s32[8]{0:T(128)} %len_hbm.1, s32[4,8]{1,0:T(4,128)} %bitcast.1), custom_call_target="tpu_custom_call" | custom-call | tf_op jit(solution)/shard_map/pallas_call | solution.py:180
  17.2 1.3 %copy.10 = bf16[1,16,128]{2,1,0:T(8,128)(2,1)} copy(bf16[1,16,128]{2,1,0:T(8,128)(2,1)} %get-tuple-element.4) | data formatting | bytes 8192
  18.4 1.4 %copy.11 = f32[8,2,512]{2,1,0:T(2,128)} copy(f32[8,2,512]{2,1,0:T(2,128)} %get-tuple-element.5) | data formatting | bytes 65536

commit v2 on v1

--- a/solution.py
+++ b/solution.py
@@ -108,6 +108,15 @@
                     here = lane_pair == pair - r * per_row
                     tops[r] = jnp.where(here, top, tops[r])
                     totals[r] = jnp.where(here, total, totals[r])
+        if codes is steps[-1]:
+            diag = (lane % group) == sub
+            for r in range(stat_rows):
+                stat[0, r:r + 1, :] = jnp.sum(jnp.where(diag, tops[r], 0.0), axis=0, keepdims=True)
+                stat[0, stat_rows + r:stat_rows + r + 1, :] = jnp.sum(
+                    jnp.where(diag, totals[r], 0.0), axis=0, keepdims=True)
+            s_sends = [to_peer(stat.at[0], stat.at[c], s_send.at[c], s_recv.at[c], c) for c in range(1, n)]
+            for copy in reversed(s_sends):
+                copy.start()
         for c in codes:
             wide = jnp.concatenate([tight[c, g] for g in range(kv)], axis=0).astype(jnp.bfloat16)
             mixed = jnp.concatenate(
@@ -117,21 +126,12 @@
                 part_out[c] = mixed
             else:
                 part_in[0] = mixed
-        if codes is steps[-1]:
-            diag = (lane % group) == sub
-            for r in range(stat_rows):
-                stat[0, r:r + 1, :] = jnp.sum(jnp.where(diag, tops[r], 0.0), axis=0, keepdims=True)
-                stat[0, stat_rows + r:stat_rows + r + 1, :] = jnp.sum(
-                    jnp.where(diag, totals[r], 0.0), axis=0, keepdims=True)
-        for c in codes:
+        for c in reversed(codes):
             if c:
                 copy = to_peer(part_out.at[c], part_in.at[c], p_send.at[c], p_recv.at[c], c)
                 copy.start()
                 p_sends.append(copy)
 
-    s_sends = [to_peer(stat.at[0], stat.at[c], s_send.at[c], s_recv.at[c], c) for c in range(1, n)]
-    for copy in reversed(s_sends):
-        copy.start()
     old_copy.wait()
     for copy in s_sends:
         copy.wait_recv()
@@ -165,6 +165,15 @@
         jnp.add, [shares[c] * part_in[c] for c in range(n)]).astype(jnp.bfloat16)
     for copy in q_sends + p_sends + s_sends:
         copy.wait_send()
+
+
+def write_out(att_ref, heavy_ref, att_out, heavy_out, sems):
+    copies = [pltpu.make_async_copy(att_ref, att_out, sems.at[0]),
+              pltpu.make_async_copy(heavy_ref, heavy_out, sems.at[1])]
+    for copy in copies:
+        copy.start()
+    for copy in copies:
+        copy.wait()
 
 
 def on_device(n, queries, keys, values, old_scores, lengths, valid_counts):
@@ -177,10 +186,10 @@
     anywhere = pl.BlockSpec(memory_space=pl.ANY)
     vmem = pl.BlockSpec(memory_space=pltpu.VMEM)
     dma = pltpu.SemaphoreType.DMA
-    return pl.pallas_call(
+    att, heavy = pl.pallas_call(
         functools.partial(kernel, n, kv, group, ctx),
-        out_shape=(jax.ShapeDtypeStruct((own, rows, hd), jnp.bfloat16),
-                   jax.ShapeDtypeStruct(old_scores.shape, jnp.float32)),
+        out_shape=(pltpu.VMEM((own, rows, hd), jnp.bfloat16),
+                   pltpu.VMEM(old_scores.shape, jnp.float32)),
         in_specs=[anywhere] * 6,
         out_specs=(vmem, vmem),
         scratch_shapes=[
@@ -199,6 +208,14 @@
         ],
         compiler_params=pltpu.CompilerParams(collective_id=0, has_side_effects=True),
     )(queries, keys, values, old_scores, lengths, counts)
+    return pl.pallas_call(
+        write_out,
+        out_shape=(jax.ShapeDtypeStruct(att.shape, att.dtype), jax.ShapeDtypeStruct(heavy.shape, heavy.dtype)),
+        in_specs=[vmem, vmem],
+        out_specs=(anywhere, anywhere),
+        scratch_shapes=[dma((2,))],
+        compiler_params=pltpu.CompilerParams(vmem_limit_bytes=2**20),
+    )(att, heavy)
 
 
 def solution(mesh):

time: 20 us -> 17 us (0.85)
  local copies, waits for them, and re-layouts: 2.65 us -> 0 us
  Pallas kernels: 16.5 us -> 16.2 us
    unnamed x2 -> x0, local copies, waits for them, and re-layouts: 2.65 us -> none
    pallas_call x1 -> x2, Pallas kernels: 16.5 us -> 16.2 us  [the longest x1 15.6 us: on_device(): pl.pallas_call(functools.partial(kernel, n, kv, group, ctx), out_shape=(p...]
where the time goes in v2:
time: 17 us; the launch traced here: 16.9 us
  Pallas kernels  16.2 us (95%)
  between operations  0.64 us (4%)
    pallas_call x1, Pallas kernels, on_device(): pl.pallas_call(functools.partial(kernel, n, kv, group, ctx), out_shape=(p...  15.6 us
    pallas_call x1, Pallas kernels, on_device(): pl.pallas_call(write_out, out_shape=(jax.ShapeDtypeStruct(att.shape, att....  0.64 us

profile of v2, /device:TPU:0, one launch (start us, length us, event | category | flops | bytes accessed | tf_op | source)
XLA Modules:
  0.0 16.9 jit_solution(3035299467405400788)
XLA Ops:
  0.6 15.6 %shard_map.77 = (bf16[1,16,128]{2,1,0:T(8,128)(2,1)S(1)}, f32[8,2,512]{2,1,0:T(2,128)S(1)}) custom-call(bf16[1,16,128]{2,1,0:T(8,128)(2,1)} %q_hbm.1, bf16[8,2,512,128]{3,2,1,0:T(8,128)(2,1)} %k_hbm.1, bf16[8,2,512,128]{3,2,1,0:T(8,128)(2,1)} %v_hbm.1, f32[8,2,512]{2,1,0:T(2,128)} %old_hbm.1, s32[8]{0:T(128)} %len_hbm.1, s32[4,8]{1,0:T(4,128)} %bitcast.1), custom_call_target="tpu_custom_call" | custom-call | tf_op jit(solution)/shard_map/pallas_call | solution.py:189
  16.2 0.6 %shard_map.78 = (bf16[1,16,128]{2,1,0:T(8,128)(2,1)}, f32[8,2,512]{2,1,0:T(2,128)}) custom-call(bf16[1,16,128]{2,1,0:T(8,128)(2,1)S(1)} %get-tuple-element.4.att_ref, f32[8,2,512]{2,1,0:T(2,128)S(1)} %get-tuple-element.5.heavy_ref), custom_call_target="tpu_custom_call" | custom-call | tf_op jit(solution)/shard_map/pallas_call | solution.py:211

commit v3 on v2

--- a/solution.py
+++ b/solution.py
@@ -36,7 +36,7 @@
     seqs = [flipped(me, c) for c in range(n)]
 
     barrier = pltpu.get_barrier_semaphore()
-    for c in range(1, n):
+    for c in reversed(range(1, n)):
         pl.semaphore_signal(barrier, inc=1, device_id={"seq": seqs[c]}, device_id_type=MESH)
 
     q_copy = pltpu.make_async_copy(q_hbm.at[0], q_all.at[0], q_dma)
@@ -76,7 +76,8 @@
     cnt_copy.wait()
     p_sends = []
     half = max(n // 2, 1)
-    steps = [list(range(0, 1)), list(range(1, half)), list(range(half, n))]
+    late = n - 1
+    steps = [list(range(0, 1)), list(range(1, half)), list(range(half, late)), list(range(late, n))]
     for codes in steps:
         for c in codes:
             if c:

time: 17 us -> 16.7 us (0.982)
  Pallas kernels: 16.2 us -> 15.9 us
    pallas_call x1, Pallas kernels: 15.6 us -> 15.2 us  [on_device(): pl.pallas_call(functools.partial(kernel, n, kv, group, ctx), out_shape=(p...]
where the time goes in v3:
time: 16.7 us; the launch traced here: 16.5 us
  Pallas kernels  15.9 us (95%)
  between operations  0.64 us (4%)
    pallas_call x1, Pallas kernels, on_device(): pl.pallas_call(functools.partial(kernel, n, kv, group, ctx), out_shape=(p...  15.2 us
    pallas_call x1, Pallas kernels, on_device(): pl.pallas_call(write_out, out_shape=(jax.ShapeDtypeStruct(att.shape, att....  0.64 us

profile of v3, /device:TPU:0, one launch (start us, length us, event | category | flops | bytes accessed | tf_op | source)
XLA Modules:
  0.0 16.5 jit_solution(12373636352581990703)
XLA Ops:
  0.6 15.2 %shard_map.77 = (bf16[1,16,128]{2,1,0:T(8,128)(2,1)S(1)}, f32[8,2,512]{2,1,0:T(2,128)S(1)}) custom-call(bf16[1,16,128]{2,1,0:T(8,128)(2,1)} %q_hbm.1, bf16[8,2,512,128]{3,2,1,0:T(8,128)(2,1)} %k_hbm.1, bf16[8,2,512,128]{3,2,1,0:T(8,128)(2,1)} %v_hbm.1, f32[8,2,512]{2,1,0:T(2,128)} %old_hbm.1, s32[8]{0:T(128)} %len_hbm.1, s32[4,8]{1,0:T(4,128)} %bitcast.1), custom_call_target="tpu_custom_call" | custom-call | tf_op jit(solution)/shard_map/pallas_call | solution.py:190
  15.9 0.6 %shard_map.78 = (bf16[1,16,128]{2,1,0:T(8,128)(2,1)}, f32[8,2,512]{2,1,0:T(2,128)}) custom-call(bf16[1,16,128]{2,1,0:T(8,128)(2,1)S(1)} %get-tuple-element.4.att_ref, f32[8,2,512]{2,1,0:T(2,128)S(1)} %get-tuple-element.5.heavy_ref), custom_call_target="tpu_custom_call" | custom-call | tf_op jit(solution)/shard_map/pallas_call | solution.py:212
